TPU v7x, 32 devices: a whole 2x2x4 slice. The times are simulated.
32 devices in a mesh: row: 16 (over z, x, core), blk: 2 (over y).
Axes of the slice: x: 2, y: 2, z: 4, core: 2. Of those that a mesh axis runs over, the one named last changes fastest.
Arguments:
- embeddings: bfloat16 [8192, 192], P(('row', 'blk')), may hold values from -30 to 30
- vectors: float32 [8192, 16], P(('row', 'blk')), may hold values from -6 to 6
Outputs:
- basis: float32 [8192, 16], P(('row', 'blk'))
- triangle: float32 [16, 16], replicated
All inputs are finite; a program needn't handle non-finite values.
Results may differ from a plain program's by a relative error of at most 0.0088.
Values may be sent and summed in bfloat16 or wider, within the bound.
A program may use at most 64 MiB of HBM per device.

v0:
```python
import jax
import jax.numpy as jnp
from jax import lax
from jax.sharding import PartitionSpec as P

sharpness = 10.0
epsilon = 1e-06


def normalize(embeddings):
    values = embeddings.astype(jnp.float32)
    return (values * lax.rsqrt(jnp.sum(values * values, axis=1, keepdims=True) + epsilon)).astype(
        jnp.bfloat16
    )


def affinity(block_rows, columns):
    scores = lax.dot_general(
        block_rows, columns, (((1,), (1,)), ((), ())), preferred_element_type=jnp.float32
    )
    return jnp.exp(sharpness * (scores - 1.0))


def gram_total(projected):
    local_gram = jnp.dot(projected.T, projected, precision=lax.Precision.HIGHEST)
    return lax.psum(local_gram, ("row", "blk"))


def finish(projected, gram_matrix):
    factor = jnp.linalg.cholesky(gram_matrix)
    basis = jax.scipy.linalg.solve_triangular(factor, projected.T, lower=True).T
    return (basis, factor.T)


def per_device(embeddings, vectors):
    unit_rows = normalize(embeddings)
    local_rows = unit_rows.shape[0]
    columns_out = vectors.shape[1]
    everything = lax.all_gather(unit_rows, ("row", "blk"), axis=0, tiled=True)
    column_blocks = everything.reshape(16, -1, everything.shape[1])

    def add_degree(running, columns):
        return (running + jnp.sum(affinity(unit_rows, columns), axis=1), None)

    degree, unused = lax.scan(add_degree, jnp.zeros((local_rows,), jnp.float32), column_blocks)
    inverse_root = lax.rsqrt(degree)
    weighted = (vectors * inverse_root[:, None]).astype(jnp.bfloat16)
    all_weighted = lax.all_gather(weighted, ("row", "blk"), axis=0, tiled=True)
    weight_blocks = all_weighted.reshape(16, -1, columns_out)

    def add_image(running, column_pair):
        tile = affinity(unit_rows, column_pair[0]).astype(jnp.bfloat16)
        return (running + jnp.dot(tile, column_pair[1], preferred_element_type=jnp.float32), None)

    summed, unused = lax.scan(
        add_image, jnp.zeros((local_rows, columns_out), jnp.float32), (column_blocks, weight_blocks)
    )
    projected = summed * inverse_root[:, None]
    gram_matrix = gram_total(projected)
    return finish(projected, gram_matrix)


def solution(mesh):
    placed = (P(("row", "blk"), None), P(("row", "blk"), None))
    return jax.shard_map(
        per_device,
        mesh=mesh,
        in_specs=placed,
        out_specs=(P(("row", "blk"), None), P()),
        check_vma=False,
    )
```

profile of v0, /device:TPU:0, one launch (start us, length us, event | category | flops | bytes accessed | tf_op | source)
XLA Modules:
  0.0 236.7 jit_solution(9475091258592382301)
XLA Ops:
  9.1 66.2 %all-gather.2.cloned.1.call-done = bf16[8192,192]{1,0:T(8,128)(2,1)} async-done(((bf16[256,192]{1,0:T(8,128)(2,1)}), bf16[8192,192]{1,0:T(8,128)(2,1)}) %all-gather.2.cloned.1.call-update) | async-done | bytes 3145744 | tf_op jit(solution)/shard_map/all_gather | solution.py:39
  75.3 21.6 %while.26 = (s32[]{:T(128)}, f32[256]{0:T(256)S(1)}, bf16[16,512,192]{2,1,0:T(8,128)(2,1)}, bf16[256,192]{1,0:T(8,128)(2,1)}, s32[]{:T(128)}, /*index=5*/s32[]{:T(128)}) while((s32[]{:T(128)}, f32[256]{0:T(256)S(1)}, bf16[16,512,192]{2,1,0:T(8,128)(2,1)}, bf16[256,192]{1,0:T(8,128)(2,1)}, s32[]{:T(128)}, /*index=5*/s32[]{:T(128)}) %tuple.72), condition=%wide.region_3.4_spmd.clone, body=%wide.region_1.3_spmd.clone.sunk | while | flops 50725120 | bytes 397903 | solution.py:45
  79.4 1.3 fusion.45
  80.7 1.3 fusion.45
  96.9 67.5 %all_gather.7 = bf16[8192,16]{0,1:T(8,128)(2,1)S(1)} all-gather(bf16[256,16]{0,1:T(8,128)(2,1)S(1)} %multiply_convert_fusion), channel_id=1, replica_groups=mesh['row'=16,'blk'=2] {'row','blk'}, dimensions={0}, use_global_device_ids=true | all-gather | bytes 270336 | tf_op jit(solution)/shard_map/all_gather | solution.py:48
  164.5 22.8 %while.27 = (s32[]{:T(128)}, f32[256,16]{0,1:T(8,128)S(1)}, bf16[16,512,192]{2,1,0:T(8,128)(2,1)}, bf16[256,192]{1,0:T(8,128)(2,1)}, bf16[16,512,16]{1,2,0:T(8,128)(2,1)S(1)}, /*index=5*/s32[]{:T(128)}, s32[]{:T(128)}) while((s32[]{:T(128)}, f32[256,16]{0,1:T(8,128)S(1)}, bf16[16,512,192]{2,1,0:T(8,128)(2,1)}, ...), condition=%wide.region_5.6_spmd.clone, body=%wide.region_4.5_spmd.clone.sunk | while | flops 54927360 | bytes 443479 | solution.py:55
  164.5 1.4 fusion.49
  165.9 1.4 fusion.49
  167.4 1.4 fusion.49
  168.8 1.4 fusion.49
  170.2 1.4 fusion.49
  171.6 1.4 fusion.49
  173.1 1.4 fusion.49
  174.5 1.4 fusion.49
  175.9 1.4 fusion.49
  177.3 1.4 fusion.49
  178.7 1.4 fusion.49
  180.2 1.4 fusion.49
  181.6 1.4 fusion.49
  183.0 1.4 fusion.49
  184.4 1.4 fusion.49
  185.9 1.4 fusion.49
  187.4 36.9 %psum.7 = f32[16,16]{0,1:T(8,128)S(1)} all-reduce(f32[16,16]{0,1:T(8,128)S(1)} %fusion.27), channel_id=1, replica_groups=mesh['row'=16,'blk'=2] {'row','blk'}, use_global_device_ids=true, to_apply=%region_6.7 | all-reduce | flops 256 | bytes 2048 | tf_op jit(solution)/shard_map/psum | solution.py:26
  224.4 1.5 cholesky.16
  (52 shorter events, 24.8 us)
Async XLA Ops:
  7.2 89.8 %copy-start = (f32[256,16]{0,1:T(8,128)S(1)}, f32[256,16]{0,1:T(8,128)}, u32[]{:S(2)}) copy-start(f32[256,16]{0,1:T(8,128)} %param.7) | copy-start | bytes 49156
  7.2 68.2 %all-gather.2.cloned.1.call-start = ((), (), s32[]{:S(2)}) async-start(), calls=%async_computation | async-start | bytes 4325376 | tf_op jit(solution)/shard_map/all_gather | solution.py:39
Sparse Core Ops, SparseCore 0:
  10.9 64.4 all-gather.1
where the time goes:
time: 238 us; the launch traced here: 237 us
  blocking collectives  104 us (44%)
  waiting for transfers between devices  66.2 us (28%)
  matrix products  44.8 us (19%)
  between operations  14.1 us (6%)
  other arithmetic  5.09 us (2%)
    all_gather x1, blocking collectives, per_device(): all_weighted = lax.all_gather(weighted, ('row', 'blk'), axis=0, tiled=True)  67.5 us
    all_gather x1, waiting for transfers between devices, per_device(): everything = lax.all_gather(unit_rows, ('row', 'blk'), axis=0, tiled=True)  66.2 us
    psum x1, blocking collectives, gram_total(): return lax.psum(local_gram, ('row', 'blk'))  36.9 us
    dot_general x16, matrix products, add_image(): jnp.dot(tile, column_pair[1], preferred_element_type=jnp.float32)  22.8 us
    dot_general x16, matrix products, affinity(): lax.dot_general(block_rows, columns, (((1,), (1,)), ((), ())), preferred_...  21.1 us
  transfers between devices with their start and end apart: 1, of which 1 were waited for; matrix products, arithmetic and copies ran while one was open for 0% of the time, Pallas kernels for 0%

commit v1 on v0

v1 whole, which is shorter than its diff:
```python
import functools
import math

import jax
import jax.numpy as jnp
from jax import lax
from jax.experimental import pallas as pl
from jax.experimental.pallas import tpu as pltpu
from jax.sharding import PartitionSpec as P

sharpness = 10.0
epsilon = 1e-06
scale2 = sharpness * math.log2(math.e)
MESH = pl.DeviceIdType.MESH
HIGH = lax.Precision.HIGHEST


def flip(bit, by):
    return bit + by - 2 * bit * by


def kernel(plane_line, emb_ref, vec_ref, basis_ref, tri_ref,
           rows, cols, aff, dpart, drecv, wts, spart, srecv, gplane, gline,
           row_s, row_r, col_s, col_r, deg_s, deg_r, wt_s, wt_r, sum_s, sum_r, gp_s, gp_r, gl_s, gl_r):
    blk_low, line = plane_line
    n_local = emb_ref.shape[1]
    r = lax.axis_index("row")
    b = lax.axis_index("blk")
    core, x, y = r % 2, (r // 2) % 2, b % 2
    z = (r // 4) * blk_low + b // 2

    def mate(t):
        c2 = flip(core, t & 1)
        x2 = flip(x, (t >> 1) & 1)
        y2 = flip(y, (t >> 2) & 1)
        return ((r // 4) * 4 + x2 * 2 + c2, (b // 2) * 2 + y2)

    def along(s):
        z2 = (z + s) % line
        return ((z2 // blk_low) * 4 + x * 2 + core, (z2 % blk_low) * 2 + y)

    barrier = pltpu.get_barrier_semaphore()
    for t in range(1, 8):
        pl.semaphore_signal(barrier, inc=1, device_id=mate(t), device_id_type=MESH)
    for s in range(1, line):
        pl.semaphore_signal(barrier, inc=1, device_id=along(s), device_id_type=MESH)

    values = emb_ref[...].astype(jnp.float32)
    norm = lax.rsqrt(jnp.sum(values * values, axis=0, keepdims=True) + epsilon)
    unit = (values * norm).astype(jnp.bfloat16)
    rows[0] = unit
    cols[0] = unit
    pl.semaphore_wait(barrier, 7 + line - 1)

    def send(src, dst, ssem, rsem, to):
        copy = pltpu.make_async_remote_copy(
            src_ref=src, dst_ref=dst, send_sem=ssem, recv_sem=rsem, device_id=to, device_id_type=MESH)
        copy.start()
        return copy

    row_copy = {}
    col_copy = {}
    order = []
    for d in range(1, line // 2 + 1):
        order.append(d)
        if line - d != d:
            order.append(line - d)
    row_copy[1] = send(rows.at[0], rows.at[1], row_s.at[1], row_r.at[1], mate(1))
    for t in (2, 4, 6):
        row_copy[t] = send(rows.at[0], rows.at[t], row_s.at[t], row_r.at[t], mate(t))
    for s in order:
        col_copy[s] = send(cols.at[0], cols.at[s], col_s.at[s], col_r.at[s], along(s))

    def tile(s, t):
        scores = lax.dot_general(cols[s], rows[t], (((0,), (0,)), ((), ())),
                                 preferred_element_type=jnp.float32)
        e = jnp.exp2(scores * scale2 - scale2)
        aff[s, t] = e.astype(jnp.bfloat16)
        part = jnp.sum(e.reshape(n_local // 8, 8, n_local), axis=0)
        return part

    def first(t):
        dpart[t] = tile(0, t)

    first(0)
    for t in (1, 2, 4, 6, 3, 5, 7):
        if t in (2, 4, 6):
            row_copy[t].wait_recv()
            row_copy[t + 1] = send(rows.at[t], rows.at[t + 1], row_s.at[t + 1], row_r.at[t + 1], mate(1))
        else:
            row_copy[t].wait_recv()
        first(t)
    for s in order:
        col_copy[s].wait_recv()

        def body(t, carry):
            dpart[t] = dpart[t] + tile(s, t)
            return carry

        lax.fori_loop(0, 8, body, 0)

    deg_copy = {}
    for t in range(8):
        drecv[8 + t] = jnp.sum(dpart[t], axis=0, keepdims=True)
    for t in range(1, 8):
        deg_copy[t] = send(drecv.at[8 + t], drecv.at[t], deg_s.at[t], deg_r.at[t], mate(t))
    eye = (lax.broadcasted_iota(jnp.int32, (16, 16), 0) == lax.broadcasted_iota(jnp.int32, (16, 16), 1))
    eyef = eye.astype(jnp.float32)
    vec_t = vec_ref[...]
    degree = drecv[8]
    for t in range(1, 8):
        deg_copy[t].wait_recv()
        degree = degree + drecv[t]
    inverse_root = lax.rsqrt(degree)
    wts[0] = (vec_t * inverse_root).astype(jnp.bfloat16)
    wt_copy = {}
    for s in order:
        wt_copy[s] = send(wts.at[0], wts.at[s], wt_s.at[s], wt_r.at[s], along(s))

    def image(s, t):
        return jnp.dot(wts[s], aff[s, t], preferred_element_type=jnp.float32)

    for t in range(8):
        spart[t] = image(0, t)
    for s in order:
        wt_copy[s].wait_recv()
        for t in range(8):
            spart[t] = spart[t] + image(s, t)
    sum_copy = {}
    for t in range(1, 8):
        sum_copy[t] = send(spart.at[t], srecv.at[t], sum_s.at[t], sum_r.at[t], mate(t))
    summed = spart[0]
    for t in range(1, 8):
        sum_copy[t].wait_recv()
        summed = summed + srecv[t]
    projected = summed * inverse_root
    gram = lax.dot_general(projected, projected, (((1,), (1,)), ((), ())), precision=HIGH,
                           preferred_element_type=jnp.float32)
    gplane[0] = gram
    gp_copy = {}
    for t in range(1, 8):
        gp_copy[t] = send(gplane.at[0], gplane.at[t], gp_s.at[t], gp_r.at[t], mate(t))
    for t in range(1, 8):
        gp_copy[t].wait_recv()
    total = ((gram + gplane[1]) + (gplane[2] + gplane[3])) + ((gplane[4] + gplane[5]) + (gplane[6] + gplane[7]))
    gline[0] = total
    gl_copy = {}
    for s in order:
        gl_copy[s] = send(gline.at[0], gline.at[s], gl_s.at[s], gl_r.at[s], along(s))
    for s in order:
        gl_copy[s].wait_recv()
    a = gline[(z + line) % line]
    for k in range(1, line):
        a = a + gline[(z + line - k) % line]

    m = eyef
    below = lax.broadcasted_iota(jnp.int32, (16, 1), 0)
    for k in range(16):
        f = jnp.where(below > k, a[:, k:k + 1] / a[k:k + 1, k:k + 1], 0.0)
        a = a - f * a[k:k + 1, :]
        m = m - f * m[k:k + 1, :]
    root = lax.rsqrt(jnp.sum(jnp.where(eye, a, 0.0), axis=1, keepdims=True))
    upper = lax.broadcasted_iota(jnp.int32, (16, 16), 0) <= lax.broadcasted_iota(jnp.int32, (16, 16), 1)
    tri_ref[...] = jnp.where(upper, a * root, 0.0)
    basis_ref[...] = jnp.dot(m * root, projected, precision=HIGH, preferred_element_type=jnp.float32)

    for group in (row_copy, col_copy, deg_copy, wt_copy, sum_copy, gp_copy, gl_copy):
        for copy in group.values():
            copy.wait_send()


def per_device(sizes, embeddings, vectors):
    blk_low, line = sizes
    n, dim = embeddings.shape
    k = vectors.shape[1]
    dma = pltpu.SemaphoreType.DMA
    vmem = pl.BlockSpec(memory_space=pltpu.VMEM)
    basis_t, tri = pl.pallas_call(
        functools.partial(kernel, sizes),
        out_shape=(jax.ShapeDtypeStruct((k, n), jnp.float32), jax.ShapeDtypeStruct((k, k), jnp.float32)),
        in_specs=[vmem, vmem],
        out_specs=(vmem, vmem),
        scratch_shapes=[
            pltpu.VMEM((8, dim, n), jnp.bfloat16),
            pltpu.VMEM((line, dim, n), jnp.bfloat16),
            pltpu.VMEM((line, 8, n, n), jnp.bfloat16),
            pltpu.VMEM((8, 8, n), jnp.float32),
            pltpu.VMEM((16, 1, n), jnp.float32),
            pltpu.VMEM((line, k, n), jnp.bfloat16),
            pltpu.VMEM((8, k, n), jnp.float32),
            pltpu.VMEM((8, k, n), jnp.float32),
            pltpu.VMEM((8, k, k), jnp.float32),
            pltpu.VMEM((line, k, k), jnp.float32),
            dma((8,)), dma((8,)), dma((line,)), dma((line,)), dma((8,)), dma((8,)),
            dma((line,)), dma((line,)), dma((8,)), dma((8,)), dma((8,)), dma((8,)),
            dma((line,)), dma((line,)),
        ],
        compiler_params=pltpu.CompilerParams(
            collective_id=0, has_side_effects=True, vmem_limit_bytes=60 * 1024 * 1024),
        name="cluster",
    )(embeddings.T, vectors.T)
    return basis_t.T, tri


def solution(mesh):
    blk_low = mesh.shape["blk"] // 2
    line = (mesh.shape["row"] // 4) * blk_low
    placed = (P(("row", "blk"), None), P(("row", "blk"), None))
    return jax.shard_map(
        functools.partial(per_device, (blk_low, line)),
        mesh=mesh,
        in_specs=placed,
        out_specs=(P(("row", "blk"), None), P()),
        check_vma=False,
    )
```

time: 238 us -> 43.5 us (0.18)
  blocking collectives: 104 us -> 0 us
  waiting for transfers between devices: 66.2 us -> 0 us
  matrix products: 44.8 us -> 0 us
  Pallas kernels: 0 us -> 40.7 us
  between operations: 14.1 us -> 0.65 us
  other arithmetic: 5.09 us -> 0 us
    all_gather x1 -> x0, blocking collectives: 67.5 us -> none  [per_device(): all_weighted = lax.all_gather(weighted, ('row', 'blk'), axis=0, tiled=True)]
    all_gather x1 -> x0, waiting for transfers between devices: 66.2 us -> none  [per_device(): everything = lax.all_gather(unit_rows, ('row', 'blk'), axis=0, tiled=True)]
    dot_general x33 -> x0, matrix products: 44 us -> none  [the longest x16 22.8 us: add_image(): jnp.dot(tile, column_pair[1], preferred_element_type=jnp.float32)]
    pallas_call x0 -> x1, Pallas kernels: none -> 40.7 us  [per_device(): pl.pallas_call(functools.partial(kernel, sizes), out_shape=(jax.ShapeDtyp...]
    psum x1 -> x0, blocking collectives: 36.9 us -> none  [gram_total(): return lax.psum(local_gram, ('row', 'blk'))]
    another operation x4 -> x0, other arithmetic: 3.36 us -> none  [the longest x3 2.13 us: finish(): factor = jnp.linalg.cholesky(gram_matrix)]
  transfers between devices with their start and end apart: 1 -> 0, of which waited for: 1 -> 0; matrix products, arithmetic and copies ran while one was open for 0% -> 0% of each run, Pallas kernels for 0% -> 0%
where the time goes in v1:
time: 43.5 us; the launch traced here: 43.3 us
  Pallas kernels  40.7 us (94%)
  local copies, waits for them, and re-layouts  1.93 us (4%)
  between operations  0.65 us (1%)
    pallas_call x1, Pallas kernels, per_device(): pl.pallas_call(functools.partial(kernel, sizes), out_shape=(jax.ShapeDtyp...  40.7 us
    unnamed x4, local copies, waits for them, and re-layouts  1.93 us

profile of v1, /device:TPU:0, one launch (start us, length us, event | category | flops | bytes accessed | tf_op | source)
XLA Modules:
  0.0 43.3 jit_solution(11568840921421777597)
XLA Ops:
  0.6 40.7 %cluster.1 = (f32[16,256]{1,0:T(8,128)}, f32[16,16]{1,0:T(8,128)}) custom-call(bf16[192,256]{1,0:T(8,128)(2,1)} %bitcast.3, f32[16,256]{1,0:T(8,128)} %bitcast.4), custom_call_target="tpu_custom_call" | custom-call | tf_op jit(solution)/shard_map/cluster/pallas_call | solution.py:178
  41.4 0.0 copy-start
  41.4 1.3 %copy.6 = f32[256,16]{0,1:T(8,128)} copy(f32[256,16]{0,1:T(8,128)} %bitcast.5) | data formatting | bytes 32768
  42.7 0.0 copy-done
  42.7 0.6 %copy.7 = f32[16,16]{1,0:T(8,128)} copy(f32[16,16]{1,0:T(8,128)S(1)} %copy-done) | data formatting | bytes 2048
Async XLA Ops:
  41.4 1.3 %copy-start = (f32[16,16]{1,0:T(8,128)S(1)}, f32[16,16]{1,0:T(8,128)}, u32[]{:S(2)}) copy-start(f32[16,16]{1,0:T(8,128)} %get-tuple-element.9) | copy-start | bytes 3076

commit v2 on v1

--- a/solution.py
+++ b/solution.py
@@ -19,7 +19,15 @@
     return bit + by - 2 * bit * by
 
 
-def kernel(plane_line, emb_ref, vec_ref, basis_ref, tri_ref,
+def split(x):
+    high = x.astype(jnp.bfloat16)
+    rest = x - high.astype(jnp.float32)
+    middle = rest.astype(jnp.bfloat16)
+    low = (rest - middle.astype(jnp.float32)).astype(jnp.bfloat16)
+    return [high, middle, low]
+
+
+def kernel(plane_line, emb_hbm, vec_hbm, basis_ref, tri_ref, emb_ref, vec_ref, in_sem,
            rows, cols, aff, dpart, drecv, wts, spart, srecv, gplane, gline,
            row_s, row_r, col_s, col_r, deg_s, deg_r, wt_s, wt_r, sum_s, sum_r, gp_s, gp_r, gl_s, gl_r):
     blk_low, line = plane_line
@@ -35,16 +43,28 @@
         y2 = flip(y, (t >> 2) & 1)
         return ((r // 4) * 4 + x2 * 2 + c2, (b // 2) * 2 + y2)
 
+    def toggled(s):
+        total, unit_bit = 0, 1
+        while unit_bit < line:
+            total = total + unit_bit * flip((z // unit_bit) % 2, (s // unit_bit) % 2)
+            unit_bit *= 2
+        return total
+
     def along(s):
-        z2 = (z + s) % line
+        z2 = toggled(s)
         return ((z2 // blk_low) * 4 + x * 2 + core, (z2 % blk_low) * 2 + y)
 
+    emb_in = pltpu.make_async_copy(emb_hbm, emb_ref, in_sem.at[0])
+    vec_in = pltpu.make_async_copy(vec_hbm, vec_ref, in_sem.at[1])
+    emb_in.start()
+    vec_in.start()
     barrier = pltpu.get_barrier_semaphore()
     for t in range(1, 8):
         pl.semaphore_signal(barrier, inc=1, device_id=mate(t), device_id_type=MESH)
     for s in range(1, line):
         pl.semaphore_signal(barrier, inc=1, device_id=along(s), device_id_type=MESH)
 
+    emb_in.wait()
     values = emb_ref[...].astype(jnp.float32)
     norm = lax.rsqrt(jnp.sum(values * values, axis=0, keepdims=True) + epsilon)
     unit = (values * norm).astype(jnp.bfloat16)
@@ -60,11 +80,7 @@
 
     row_copy = {}
     col_copy = {}
-    order = []
-    for d in range(1, line // 2 + 1):
-        order.append(d)
-        if line - d != d:
-            order.append(line - d)
+    order = list(range(1, line))
     row_copy[1] = send(rows.at[0], rows.at[1], row_s.at[1], row_r.at[1], mate(1))
     for t in (2, 4, 6):
         row_copy[t] = send(rows.at[0], rows.at[t], row_s.at[t], row_r.at[t], mate(t))
@@ -106,6 +122,7 @@
         deg_copy[t] = send(drecv.at[8 + t], drecv.at[t], deg_s.at[t], deg_r.at[t], mate(t))
     eye = (lax.broadcasted_iota(jnp.int32, (16, 16), 0) == lax.broadcasted_iota(jnp.int32, (16, 16), 1))
     eyef = eye.astype(jnp.float32)
+    vec_in.wait()
     vec_t = vec_ref[...]
     degree = drecv[8]
     for t in range(1, 8):
@@ -134,8 +151,11 @@
         sum_copy[t].wait_recv()
         summed = summed + srecv[t]
     projected = summed * inverse_root
-    gram = lax.dot_general(projected, projected, (((1,), (1,)), ((), ())), precision=HIGH,
-                           preferred_element_type=jnp.float32)
+    pieces = jnp.concatenate(split(projected), axis=0)
+    products = lax.dot_general(pieces, pieces, (((1,), (1,)), ((), ())),
+                               preferred_element_type=jnp.float32)
+    halves = products[0:16] + products[16:32] + products[32:48]
+    gram = halves[:, 0:16] + halves[:, 16:32] + halves[:, 32:48]
     gplane[0] = gram
     gp_copy = {}
     for t in range(1, 8):
@@ -149,9 +169,10 @@
         gl_copy[s] = send(gline.at[0], gline.at[s], gl_s.at[s], gl_r.at[s], along(s))
     for s in order:
         gl_copy[s].wait_recv()
-    a = gline[(z + line) % line]
-    for k in range(1, line):
-        a = a + gline[(z + line - k) % line]
+    terms = [gline[s] for s in range(line)]
+    while len(terms) > 1:
+        terms = [terms[k] + terms[k + 1] for k in range(0, len(terms), 2)]
+    a = terms[0]
 
     m = eyef
     below = lax.broadcasted_iota(jnp.int32, (16, 1), 0)
@@ -178,9 +199,12 @@
     basis_t, tri = pl.pallas_call(
         functools.partial(kernel, sizes),
         out_shape=(jax.ShapeDtypeStruct((k, n), jnp.float32), jax.ShapeDtypeStruct((k, k), jnp.float32)),
-        in_specs=[vmem, vmem],
+        in_specs=[pl.BlockSpec(memory_space=pl.ANY)] * 2,
         out_specs=(vmem, vmem),
         scratch_shapes=[
+            pltpu.VMEM((dim, n), jnp.bfloat16),
+            pltpu.VMEM((k, n), jnp.float32),
+            dma((2,)),
             pltpu.VMEM((8, dim, n), jnp.bfloat16),
             pltpu.VMEM((line, dim, n), jnp.bfloat16),
             pltpu.VMEM((line, 8, n, n), jnp.bfloat16),

time: 43.5 us -> 41.8 us (0.961)
  Pallas kernels: 40.7 us -> 39 us
    pallas_call x1, Pallas kernels: 40.7 us -> 39 us  [per_device(): pl.pallas_call(functools.partial(kernel, sizes), out_shape=(jax.ShapeDtyp...]
where the time goes in v2:
time: 41.8 us; the launch traced here: 41.6 us
  Pallas kernels  39 us (93%)
  local copies, waits for them, and re-layouts  1.93 us (5%)
  between operations  0.65 us (2%)
    pallas_call x1, Pallas kernels, per_device(): pl.pallas_call(functools.partial(kernel, sizes), out_shape=(jax.ShapeDtyp...  39 us
    unnamed x4, local copies, waits for them, and re-layouts  1.93 us

profile of v2, /device:TPU:0, one launch (start us, length us, event | category | flops | bytes accessed | tf_op | source)
XLA Modules:
  0.0 41.6 jit_solution(8204564343475504169)
XLA Ops:
  0.6 39.0 %cluster.1 = (f32[16,256]{1,0:T(8,128)}, f32[16,16]{1,0:T(8,128)}) custom-call(bf16[192,256]{1,0:T(8,128)(2,1)} %bitcast.3, f32[16,256]{1,0:T(8,128)} %bitcast.4), custom_call_target="tpu_custom_call" | custom-call | tf_op jit(solution)/shard_map/cluster/pallas_call | solution.py:199
  39.7 0.0 copy-start
  39.7 1.3 %copy.6 = f32[256,16]{0,1:T(8,128)} copy(f32[256,16]{0,1:T(8,128)} %bitcast.5) | data formatting | bytes 32768
  41.0 0.0 copy-done
  41.0 0.6 %copy.7 = f32[16,16]{1,0:T(8,128)} copy(f32[16,16]{1,0:T(8,128)S(1)} %copy-done) | data formatting | bytes 2048
Async XLA Ops:
  39.7 1.3 %copy-start = (f32[16,16]{1,0:T(8,128)S(1)}, f32[16,16]{1,0:T(8,128)}, u32[]{:S(2)}) copy-start(f32[16,16]{1,0:T(8,128)} %get-tuple-element.9) | copy-start | bytes 3076

commit v3 on v2

--- a/solution.py
+++ b/solution.py
@@ -28,7 +28,7 @@
 
 
 def kernel(plane_line, emb_hbm, vec_hbm, basis_ref, tri_ref, emb_ref, vec_ref, in_sem,
-           rows, cols, aff, dpart, drecv, wts, spart, srecv, gplane, gline,
+           rows, cols, turned, aff, dpart, drecv, wts, spart, srecv, gplane, gline,
            row_s, row_r, col_s, col_r, deg_s, deg_r, wt_s, wt_r, sum_s, sum_r, gp_s, gp_r, gl_s, gl_r):
     blk_low, line = plane_line
     n_local = emb_ref.shape[1]
@@ -88,12 +88,16 @@
         col_copy[s] = send(cols.at[0], cols.at[s], col_s.at[s], col_r.at[s], along(s))
 
     def tile(s, t):
-        scores = lax.dot_general(cols[s], rows[t], (((0,), (0,)), ((), ())),
-                                 preferred_element_type=jnp.float32)
+        scores = jnp.dot(turned[s], rows[t], preferred_element_type=jnp.float32)
         e = jnp.exp2(scores * scale2 - scale2)
         aff[s, t] = e.astype(jnp.bfloat16)
         part = jnp.sum(e.reshape(n_local // 8, 8, n_local), axis=0)
         return part
+
+    def turn(s):
+        turned[s] = cols[s].astype(jnp.float32).T.astype(jnp.bfloat16)
+
+    turn(0)
 
     def first(t):
         dpart[t] = tile(0, t)
@@ -108,12 +112,13 @@
         first(t)
     for s in order:
         col_copy[s].wait_recv()
+        turn(s)
 
         def body(t, carry):
             dpart[t] = dpart[t] + tile(s, t)
             return carry
 
-        lax.fori_loop(0, 8, body, 0)
+        lax.fori_loop(0, 8, body, 0, unroll=8 if line <= 8 else 1)
 
     deg_copy = {}
     for t in range(8):
@@ -156,6 +161,7 @@
                                preferred_element_type=jnp.float32)
     halves = products[0:16] + products[16:32] + products[32:48]
     gram = halves[:, 0:16] + halves[:, 16:32] + halves[:, 32:48]
+    gram = jnp.concatenate([gram[0:8], gram[8:16]], axis=1)
     gplane[0] = gram
     gp_copy = {}
     for t in range(1, 8):
@@ -172,7 +178,7 @@
     terms = [gline[s] for s in range(line)]
     while len(terms) > 1:
         terms = [terms[k] + terms[k + 1] for k in range(0, len(terms), 2)]
-    a = terms[0]
+    a = jnp.concatenate([terms[0][:, 0:16], terms[0][:, 16:32]], axis=0)
 
     m = eyef
     below = lax.broadcasted_iota(jnp.int32, (16, 1), 0)
@@ -207,14 +213,15 @@
             dma((2,)),
             pltpu.VMEM((8, dim, n), jnp.bfloat16),
             pltpu.VMEM((line, dim, n), jnp.bfloat16),
+            pltpu.VMEM((line, n, dim), jnp.bfloat16),
             pltpu.VMEM((line, 8, n, n), jnp.bfloat16),
             pltpu.VMEM((8, 8, n), jnp.float32),
             pltpu.VMEM((16, 1, n), jnp.float32),
             pltpu.VMEM((line, k, n), jnp.bfloat16),
             pltpu.VMEM((8, k, n), jnp.float32),
             pltpu.VMEM((8, k, n), jnp.float32),
-            pltpu.VMEM((8, k, k), jnp.float32),
-            pltpu.VMEM((line, k, k), jnp.float32),
+            pltpu.VMEM((8, k // 2, 2 * k), jnp.float32),
+            pltpu.VMEM((line, k // 2, 2 * k), jnp.float32),
             dma((8,)), dma((8,)), dma((line,)), dma((line,)), dma((8,)), dma((8,)),
             dma((line,)), dma((line,)), dma((8,)), dma((8,)), dma((8,)), dma((8,)),
             dma((line,)), dma((line,)),

time: 41.8 us -> 38.8 us (0.928)
  Pallas kernels: 39 us -> 36.1 us
    pallas_call x1, Pallas kernels: 39 us -> 36.1 us  [per_device(): pl.pallas_call(functools.partial(kernel, sizes), out_shape=(jax.ShapeDtyp...]
where the time goes in v3:
time: 38.8 us; the launch traced here: 38.6 us
  Pallas kernels  36.1 us (93%)
  local copies, waits for them, and re-layouts  1.93 us (5%)
  between operations  0.65 us (2%)
    pallas_call x1, Pallas kernels, per_device(): pl.pallas_call(functools.partial(kernel, sizes), out_shape=(jax.ShapeDtyp...  36.1 us
    unnamed x4, local copies, waits for them, and re-layouts  1.93 us

profile of v3, /device:TPU:0, one launch (start us, length us, event | category | flops | bytes accessed | tf_op | source)
XLA Modules:
  0.0 38.6 jit_solution(12159904828047198684)
XLA Ops:
  0.6 36.1 %cluster.1 = (f32[16,256]{1,0:T(8,128)}, f32[16,16]{1,0:T(8,128)}) custom-call(bf16[192,256]{1,0:T(8,128)(2,1)} %bitcast.3, f32[16,256]{1,0:T(8,128)} %bitcast.4), custom_call_target="tpu_custom_call" | custom-call | tf_op jit(solution)/shard_map/cluster/pallas_call | solution.py:205
  36.7 0.0 copy-start
  36.7 1.3 %copy.6 = f32[256,16]{0,1:T(8,128)} copy(f32[256,16]{0,1:T(8,128)} %bitcast.5) | data formatting | bytes 32768
  38.0 0.0 copy-done
  38.0 0.6 %copy.7 = f32[16,16]{1,0:T(8,128)} copy(f32[16,16]{1,0:T(8,128)S(1)} %copy-done) | data formatting | bytes 2048
Async XLA Ops:
  36.7 1.3 %copy-start = (f32[16,16]{1,0:T(8,128)S(1)}, f32[16,16]{1,0:T(8,128)}, u32[]{:S(2)}) copy-start(f32[16,16]{1,0:T(8,128)} %get-tuple-element.9) | copy-start | bytes 3076

commit v4 on v3

--- a/solution.py
+++ b/solution.py
@@ -84,8 +84,21 @@
     row_copy[1] = send(rows.at[0], rows.at[1], row_s.at[1], row_r.at[1], mate(1))
     for t in (2, 4, 6):
         row_copy[t] = send(rows.at[0], rows.at[t], row_s.at[t], row_r.at[t], mate(t))
-    for s in order:
-        col_copy[s] = send(cols.at[0], cols.at[s], col_s.at[s], col_r.at[s], along(s))
+    relayed = line == 4
+    half = cols.shape[1] // 2
+
+    def send_part(key, source, slot, start, to):
+        part = pl.ds(start, half)
+        col_copy[key] = send(cols.at[source, part], cols.at[slot, part], col_s.at[key], col_r.at[key], to)
+
+    if relayed:
+        send_part(2, 0, 2, 0, along(2))
+        send_part(4, 0, 2, half, along(2))
+        col_copy[1] = send(cols.at[0], cols.at[1], col_s.at[1], col_r.at[1], along(1))
+        send_part(3, 0, 3, half, along(3))
+    else:
+        for s in order:
+            col_copy[s] = send(cols.at[0], cols.at[s], col_s.at[s], col_r.at[s], along(s))
 
     def tile(s, t):
         scores = jnp.dot(turned[s], rows[t], preferred_element_type=jnp.float32)
@@ -104,6 +117,9 @@
 
     first(0)
     for t in (1, 2, 4, 6, 3, 5, 7):
+        if relayed and t == 6:
+            col_copy[2].wait_recv()
+            send_part(5, 2, 3, 0, along(1))
         if t in (2, 4, 6):
             row_copy[t].wait_recv()
             row_copy[t + 1] = send(rows.at[t], rows.at[t + 1], row_s.at[t + 1], row_r.at[t + 1], mate(1))
@@ -111,7 +127,14 @@
             row_copy[t].wait_recv()
         first(t)
     for s in order:
-        col_copy[s].wait_recv()
+        if relayed and s > 1:
+            if s == 2:
+                col_copy[4].wait_recv()
+            else:
+                col_copy[3].wait_recv()
+                col_copy[5].wait_recv()
+        else:
+            col_copy[s].wait_recv()
         turn(s)
 
         def body(t, carry):
@@ -222,7 +245,7 @@
             pltpu.VMEM((8, k, n), jnp.float32),
             pltpu.VMEM((8, k // 2, 2 * k), jnp.float32),
             pltpu.VMEM((line, k // 2, 2 * k), jnp.float32),
-            dma((8,)), dma((8,)), dma((line,)), dma((line,)), dma((8,)), dma((8,)),
+            dma((8,)), dma((8,)), dma((line + 2,)), dma((line + 2,)), dma((8,)), dma((8,)),
             dma((line,)), dma((line,)), dma((8,)), dma((8,)), dma((8,)), dma((8,)),
             dma((line,)), dma((line,)),
         ],

time: 38.8 us -> 38.2 us (0.985)
  Pallas kernels: 36.1 us -> 35.4 us
    pallas_call x1, Pallas kernels: 36.1 us -> 35.4 us  [per_device(): pl.pallas_call(functools.partial(kernel, sizes), out_shape=(jax.ShapeDtyp...]
where the time goes in v4:
time: 38.2 us; the launch traced here: 38 us
  Pallas kernels  35.4 us (93%)
  local copies, waits for them, and re-layouts  1.93 us (5%)
  between operations  0.65 us (2%)
    pallas_call x1, Pallas kernels, per_device(): pl.pallas_call(functools.partial(kernel, sizes), out_shape=(jax.ShapeDtyp...  35.4 us
    unnamed x4, local copies, waits for them, and re-layouts  1.93 us

profile of v4, /device:TPU:0, one launch (start us, length us, event | category | flops | bytes accessed | tf_op | source)
XLA Modules:
  0.0 38.0 jit_solution(14452250505313681868)
XLA Ops:
  0.6 35.4 %cluster.1 = (f32[16,256]{1,0:T(8,128)}, f32[16,16]{1,0:T(8,128)}) custom-call(bf16[192,256]{1,0:T(8,128)(2,1)} %bitcast.3, f32[16,256]{1,0:T(8,128)} %bitcast.4), custom_call_target="tpu_custom_call" | custom-call | tf_op jit(solution)/shard_map/cluster/pallas_call | solution.py:228
  36.0 0.0 copy-start
  36.0 1.3 %copy.6 = f32[256,16]{0,1:T(8,128)} copy(f32[256,16]{0,1:T(8,128)} %bitcast.5) | data formatting | bytes 32768
  37.4 0.0 copy-done
  37.4 0.6 %copy.7 = f32[16,16]{1,0:T(8,128)} copy(f32[16,16]{1,0:T(8,128)S(1)} %copy-done) | data formatting | bytes 2048
Async XLA Ops:
  36.0 1.3 %copy-start = (f32[16,16]{1,0:T(8,128)S(1)}, f32[16,16]{1,0:T(8,128)}, u32[]{:S(2)}) copy-start(f32[16,16]{1,0:T(8,128)} %get-tuple-element.9) | copy-start | bytes 3076

commit v5 on v4

--- a/solution.py
+++ b/solution.py
@@ -167,13 +167,17 @@
 
     for t in range(8):
         spart[t] = image(0, t)
+    sum_copy = {}
     for s in order:
         wt_copy[s].wait_recv()
-        for t in range(8):
+        ready = None
+        for t in (1, 2, 3, 4, 5, 6, 7, 0):
             spart[t] = spart[t] + image(s, t)
-    sum_copy = {}
-    for t in range(1, 8):
-        sum_copy[t] = send(spart.at[t], srecv.at[t], sum_s.at[t], sum_r.at[t], mate(t))
+            if s == order[-1]:
+                if ready is not None:
+                    sum_copy[ready] = send(
+                        spart.at[ready], srecv.at[ready], sum_s.at[ready], sum_r.at[ready], mate(ready))
+                ready = t
     summed = spart[0]
     for t in range(1, 8):
         sum_copy[t].wait_recv()

time: 38.2 us -> 38.4 us (level)
  no operation moved by 1% of the time
where the time goes in v5:
time: 38.4 us; the launch traced here: 38.2 us
  Pallas kernels  35.7 us (93%)
  local copies, waits for them, and re-layouts  1.93 us (5%)
  between operations  0.65 us (2%)
    pallas_call x1, Pallas kernels, per_device(): pl.pallas_call(functools.partial(kernel, sizes), out_shape=(jax.ShapeDtyp...  35.7 us
    unnamed x4, local copies, waits for them, and re-layouts  1.93 us

profile of v5, /device:TPU:0, one launch (start us, length us, event | category | flops | bytes accessed | tf_op | source)
XLA Modules:
  0.0 38.2 jit_solution(14659208692938359478)
XLA Ops:
  0.6 35.7 %cluster.1 = (f32[16,256]{1,0:T(8,128)}, f32[16,16]{1,0:T(8,128)}) custom-call(bf16[192,256]{1,0:T(8,128)(2,1)} %bitcast.3, f32[16,256]{1,0:T(8,128)} %bitcast.4), custom_call_target="tpu_custom_call" | custom-call | tf_op jit(solution)/shard_map/cluster/pallas_call | solution.py:232
  36.3 0.0 copy-start
  36.3 1.3 %copy.6 = f32[256,16]{0,1:T(8,128)} copy(f32[256,16]{0,1:T(8,128)} %bitcast.5) | data formatting | bytes 32768
  37.6 0.0 copy-done
  37.6 0.6 %copy.7 = f32[16,16]{1,0:T(8,128)} copy(f32[16,16]{1,0:T(8,128)S(1)} %copy-done) | data formatting | bytes 2048
Async XLA Ops:
  36.3 1.3 %copy-start = (f32[16,16]{1,0:T(8,128)S(1)}, f32[16,16]{1,0:T(8,128)}, u32[]{:S(2)}) copy-start(f32[16,16]{1,0:T(8,128)} %get-tuple-element.9) | copy-start | bytes 3076
